TPU v7x, 32 devices: a whole 2x2x4 slice. The times are simulated.
32 devices in a mesh: kx: 8 (over z, x), cz: 4 (over y, core).
Axes of the slice: x: 2, y: 2, z: 4, core: 2. Of those that a mesh axis runs over, the one named last changes fastest.
Arguments:
- field_modes: bfloat16 [512, 4, 12288], P('cz', None, 'kx'), may hold values from -6 to 6
- cotangent: bfloat16 [512, 4, 12288], P('cz', None, 'kx'), may hold values from -6 to 6
Outputs:
- mode_gradient: bfloat16 [512, 4, 12288], P('cz', None, 'kx')
All inputs are finite; a program needn't handle non-finite values.
Results may differ from a plain program's by a relative error of at most 0.009.
Values may be sent and summed in bfloat16 or wider, within the bound.
A program may use at most 128 MiB of HBM per device.

v0:
```python
import math
import jax
import jax.numpy as jnp
from jax import lax
from jax.sharding import PartitionSpec as P

NZ = 512
MZ = 768
NX = 768
Y = 16


def cosine_table():
    row_index = jnp.arange(MZ, dtype=jnp.int32)
    col_index = jnp.arange(NZ, dtype=jnp.int32)
    position = col_index[None, :] * (2 * row_index[:, None] + 1) % (4 * MZ)
    return jnp.cos(jnp.pi * position.astype(jnp.float32) / (2 * MZ))


def hartley_table():
    points = jnp.arange(NX, dtype=jnp.int32)
    position = points[:, None] * points[None, :] % NX
    phases = 2.0 * jnp.pi * position.astype(jnp.float32) / NX
    return ((jnp.cos(phases) + jnp.sin(phases)) / math.sqrt(NX)).astype(jnp.bfloat16)


def product_gradient(fields, adjoint):
    vertical = fields[2]
    return jnp.stack(
        [
            adjoint[0] * vertical,
            adjoint[1] * vertical,
            adjoint[0] * fields[0]
            + adjoint[1] * fields[1]
            + 2.0 * adjoint[2] * vertical
            + adjoint[3] * fields[3],
            adjoint[3] * vertical,
        ]
    ).astype(jnp.bfloat16)


def on_device(field_modes, cotangent):
    local_modes = field_modes.shape[0]
    field_count = field_modes.shape[1]
    local_columns = field_modes.shape[2] // Y
    field_grid = field_modes.reshape(local_modes, field_count, local_columns, Y)
    cotangent_grid = cotangent.reshape(local_modes, field_count, local_columns, Y)
    cosines = cosine_table()
    synthesis = (cosines * math.sqrt(2.0 / NZ)).astype(jnp.bfloat16)
    projection = (cosines * math.sqrt(2.0 / MZ)).astype(jnp.bfloat16)
    hartley = hartley_table()
    lifted = jnp.concatenate(
        [
            jnp.einsum(
                "zk,kfxy->yfxz",
                synthesis,
                lax.all_to_all(field_grid, "cz", split_axis=3, concat_axis=0, tiled=True),
                preferred_element_type=jnp.float32,
            ).astype(jnp.bfloat16),
            jnp.einsum(
                "zk,kfxy->yfxz",
                projection,
                lax.all_to_all(cotangent_grid, "cz", split_axis=3, concat_axis=0, tiled=True),
                preferred_element_type=jnp.float32,
            ).astype(jnp.bfloat16),
        ],
        axis=1,
    )
    piece = lax.all_to_all(lifted, "kx", split_axis=3, concat_axis=2, tiled=True)
    fields = jnp.einsum(
        "xm,yfmz->fyzx", hartley, piece[:, :field_count], preferred_element_type=jnp.float32
    )
    adjoint = jnp.einsum(
        "xm,yfmz->fyzx", hartley, piece[:, field_count:], preferred_element_type=jnp.float32
    )
    gradient = product_gradient(fields, adjoint)
    turned = jnp.einsum(
        "xm,fyzx->yfmz", hartley, gradient, preferred_element_type=jnp.float32
    ).astype(jnp.bfloat16)
    returned = lax.all_to_all(turned, "kx", split_axis=2, concat_axis=3, tiled=True)
    spectral = jnp.einsum(
        "zk,yfxz->kfxy", synthesis, returned, preferred_element_type=jnp.float32
    ).astype(jnp.bfloat16)
    result = lax.all_to_all(spectral, "cz", split_axis=0, concat_axis=3, tiled=True)
    return result.reshape(local_modes, field_count, local_columns * Y)


def solution(mesh):
    return jax.shard_map(
        on_device,
        mesh=mesh,
        in_specs=(P("cz", None, "kx"), P("cz", None, "kx")),
        out_specs=P("cz", None, "kx"),
        check_vma=False,
    )
```

profile of v0, /device:TPU:0, one launch (start us, length us, event | category | flops | bytes accessed | tf_op | source)
XLA Modules:
  0.0 435.8 jit_solution(16268019331299790281)
XLA Ops:
  0.0 3.0 copy.18
  3.0 1.6 copy.19
  4.5 4.3 all-to-all-start
  8.8 3.0 copy.22
  11.7 1.6 copy.23
  13.3 15.5 %all-to-all-done = bf16[128,4,96,16]{0,2,1,3:T(8,128)(2,1)S(1)} async-done(((bf16[128,4,96,16]{0,2,1,3:T(8,128)(2,1)}), bf16[128,4,96,16]{0,2,1,3:T(8,128)(2,1)S(1)}, u32[]{:S(2)}, u32[]{:S(2)}) %all-to-all-start) | async-done | bytes 1572896 | tf_op jit(solution)/shard_map/all_to_all | solution.py:57
  28.8 3.6 all-to-all-start.1
  32.4 2.4 copy.21
  34.8 3.6 all_to_all.66
  38.4 14.0 %all-to-all-done.1 = bf16[128,4,96,16]{0,2,1,3:T(8,128)(2,1)S(1)} async-done(((bf16[128,4,96,16]{0,2,1,3:T(8,128)(2,1)}), bf16[128,4,96,16]{0,2,1,3:T(8,128)(2,1)S(1)}, u32[]{:S(2)}, u32[]{:S(2)}) %all-to-all-start.1) | async-done | bytes 1572896 | tf_op jit(solution)/shard_map/all_to_all | solution.py:63
  52.4 1.2 copy.25
  53.6 2.0 all_to_all.70
  55.6 9.7 %convert_bitcast_fusion.2 = bf16[4,4,96,768]{3,2,0,1:T(8,128)(2,1)S(1)} fusion(bf16[512,4,96,4]{0,2,3,1:T(8,128)(2,1)S(1)} %copy-done.1, s32[768]{0:T(1024)S(1)} %multiply_add_fusion), kind=kOutput, calls=%fused_computation.16 | convolution fusion | flops 1213464576 | bytes 3935232 | tf_op jit(solution)/shard_map/zk,kfxy->yfxz/dot_general | solution.py:54
  65.4 9.7 %convert_bitcast_fusion.1 = bf16[4,4,96,768]{3,2,0,1:T(8,128)(2,1)S(1)} fusion(bf16[512,4,96,4]{0,2,3,1:T(8,128)(2,1)S(1)} %copy-done.2, s32[768]{0:T(1024)S(1)} %multiply_add_fusion), kind=kOutput, calls=%fused_computation.15 | convolution fusion | flops 1213464576 | bytes 3935232 | tf_op jit(solution)/shard_map/zk,kfxy->yfxz/dot_general | solution.py:60
  75.1 2.6 pad_maximum_fusion
  77.7 10.9 %copy.26 = bf16[4,8,96,768]{2,0,1,3:T(4,128)(2,1)} copy(bf16[4,8,96,768]{3,2,0,1:T(8,128)(2,1)} %pad_maximum_fusion) | data formatting | bytes 9437184 | tf_op jit(solution)/shard_map/concatenate | solution.py:52
  88.7 144.9 %all_to_all.87 = bf16[4,8,96,768]{2,0,1,3:T(4,128)(2,1)S(1)} all-to-all(bf16[4,8,96,768]{2,0,1,3:T(4,128)(2,1)} %copy.26), channel_id=1, replica_groups=mesh['kx'=8,'cz'=4] {'kx'}, dimensions={3} | all-to-all | bytes 9437184 | tf_op jit(solution)/shard_map/all_to_all | solution.py:69
  233.6 6.7 %copy.45 = bf16[4,8,96,8,96]{2,3,4,1,0:T(8,128)(2,1)} copy(bf16[4,8,96,8,96]{2,0,1,4,3:T(4,128)(2,1)S(1)} %bitcast.65) | data formatting | bytes 9437184 | tf_op jit(solution)/shard_map/all_to_all | solution.py:69
  240.3 10.8 %all_to_all.74 = bf16[4,8,768,96]{2,3,1,0:T(8,128)(2,1)} reshape(bf16[4,8,8,96,96]{3,2,4,1,0:T(8,128)(2,1)} %bitcast.66) | data formatting | bytes 9437184 | tf_op jit(solution)/shard_map/all_to_all | solution.py:69
  251.1 12.7 %convolution_bitcast_fusion = f32[4,4,96,768]{3,2,0,1:T(8,128)S(1)} fusion(bf16[4,8,768,96]{2,3,1,0:T(8,128)(2,1)} %all_to_all.74), kind=kOutput, calls=%fused_computation.18 | convolution fusion | flops 1819017216 | bytes 9437184 | tf_op jit(solution)/shard_map/xm,yfmz->fyzx/dot_general | solution.py:70
  263.8 25.5 %convolution_bitcast_fusion.1 = f32[4,4,96,768]{3,2,0,1:T(8,128)S(1)} fusion(bf16[4,8,768,96]{2,3,1,0:T(8,128)(2,1)S(1)} %copy-done), kind=kOutput, calls=%fused_computation.19 | convolution fusion | flops 1819017216 | bytes 9437184 | tf_op jit(solution)/shard_map/xm,yfmz->fyzx/dot_general | solution.py:73
  289.3 0.9 multiply_convert_fusion.5
  290.2 12.3 %convert_bitcast_fusion = bf16[4,4,768,96]{2,3,0,1:T(8,128)(2,1)} fusion(bf16[1,4,96,768]{3,2,0,1:T(8,128)(2,1)S(1)} %get-tuple-element.6, bf16[1,4,96,768]{3,2,0,1:T(8,128)(2,1)S(1)} %get-tuple-element.7, bf16[1,4,96,768]{3,2,0,1:T(8,128)(2,1)S(1)} %get-tuple-element.8, bf16[1,4,96,768]{3,2,0,1:T(8,128)(2,1)S(1)} %get-tuple-element.5), kind=kOutput, calls=%fused_computation.10 | convolution fusion | flops 1823735808 | bytes 4718592 | tf_op jit(solution)/shard_map/xm,fyzx->yfmz/dot_general | solution.py:77
  302.5 5.0 %copy.29 = bf16[4,4,768,96]{3,0,1,2:T(4,128)(2,1)S(1)} copy(bf16[4,4,768,96]{2,3,0,1:T(8,128)(2,1)} %convert_bitcast_fusion) | data formatting | bytes 4718592 | tf_op jit(solution)/shard_map/convert_element_type | solution.py:79
  307.5 73.6 %all_to_all.88 = bf16[4,4,768,96]{3,0,1,2:T(4,128)(2,1)S(1)} all-to-all(bf16[4,4,768,96]{3,0,1,2:T(4,128)(2,1)S(1)} %copy.29), channel_id=1, replica_groups=mesh['kx'=8,'cz'=4] {'kx'}, dimensions={2} | all-to-all | bytes 4718592 | tf_op jit(solution)/shard_map/all_to_all | solution.py:80
  381.1 2.0 copy.46
  383.1 3.6 all_to_all.78
  386.7 9.9 %fusion.15 = bf16[512,4,96,4]{0,2,1,3:T(8,128)(2,1)} fusion(bf16[4,4,96,768]{3,2,1,0:T(8,128)(2,1)} %all_to_all.78, s32[768]{0:T(1024)S(1)} %multiply_add_fusion), kind=kOutput, calls=%fused_computation.30 | convolution fusion | flops 1213071360 | bytes 3935232 | tf_op jit(solution)/shard_map/zk,yfxz->kfxy/dot_general | solution.py:81
  396.6 3.3 copy.31
  400.0 28.9 %all_to_all.89 = bf16[512,4,96,4]{2,1,3,0:T(4,128)(2,1)} all-to-all(bf16[512,4,96,4]{2,1,3,0:T(4,128)(2,1)S(1)} %copy.31), channel_id=1, replica_groups=mesh['kx'=8,'cz'=4] {'cz'}, dimensions={0} | all-to-all | bytes 3145728 | tf_op jit(solution)/shard_map/all_to_all | solution.py:84
  428.9 4.0 copy.32
  432.9 2.5 copy.33
  (7 shorter events, 0.0 us)
Async XLA Ops:
  4.5 24.3 %all-to-all-start = ((bf16[128,4,96,16]{0,2,1,3:T(8,128)(2,1)}), bf16[128,4,96,16]{0,2,1,3:T(8,128)(2,1)S(1)}, u32[]{:S(2)}, u32[]{:S(2)}) async-start(bf16[128,4,96,16]{0,2,1,3:T(8,128)(2,1)} %copy.19), calls=%async_computation | async-start | bytes 3145728 | tf_op jit(solution)/shard_map/all_to_all | solution.py:57
  28.8 23.6 %all-to-all-start.1 = ((bf16[128,4,96,16]{0,2,1,3:T(8,128)(2,1)}), bf16[128,4,96,16]{0,2,1,3:T(8,128)(2,1)S(1)}, u32[]{:S(2)}, u32[]{:S(2)}) async-start(bf16[128,4,96,16]{0,2,1,3:T(8,128)(2,1)} %copy.23), calls=%async_computation.1 | async-start | bytes 3145728 | tf_op jit(solution)/shard_map/all_to_all | solution.py:63
  53.6 2.0 copy-start.1
  55.6 9.7 %copy-start.2 = (bf16[512,4,96,4]{0,2,3,1:T(8,128)(2,1)S(1)}, bf16[512,4,96,4]{0,2,3,1:T(8,128)(2,1)}, u32[]{:S(2)}) copy-start(bf16[512,4,96,4]{0,2,3,1:T(8,128)(2,1)} %all_to_all.70) | copy-start | bytes 4718596
  251.1 12.7 %copy-start = (bf16[4,8,768,96]{2,3,1,0:T(8,128)(2,1)S(1)}, bf16[4,8,768,96]{2,3,1,0:T(8,128)(2,1)}, u32[]{:S(2)}) copy-start(bf16[4,8,768,96]{2,3,1,0:T(8,128)(2,1)} %all_to_all.74) | copy-start | bytes 14155780
where the time goes:
time: 444 us; the launch traced here: 436 us
  blocking collectives  247 us (56%)
  matrix products  79.8 us (18%)
  local copies, waits for them, and re-layouts  67.2 us (15%)
  waiting for transfers between devices  29.5 us (7%)
  starting transfers between devices  7.83 us (2%)
    all_to_all x1, blocking collectives, on_device(): lax.all_to_all(lifted, 'kx', split_axis=3, concat_axis=2, tiled=True)  145 us
    all_to_all x1, blocking collectives, on_device(): lax.all_to_all(turned, 'kx', split_axis=2, concat_axis=3, tiled=True)  73.6 us
    all_to_all x1, blocking collectives, on_device(): lax.all_to_all(spectral, 'cz', split_axis=0, concat_axis=3, tiled=True)  28.9 us
    dot_general x1, matrix products, on_device(): jnp.einsum('xm,yfmz->fyzx', hartley, piece[:, field_count:], preferred_el...  25.5 us
    all_to_all x2, local copies, waits for them, and re-layouts, on_device(): lax.all_to_all(lifted, 'kx', split_axis=3, concat_axis=2, tiled=True)  17.5 us
    all_to_all x1, waiting for transfers between devices, on_device(): lax.all_to_all(field_grid, 'cz', split_axis=3, concat_axis=0, tiled=True)  15.5 us
    all_to_all x1, waiting for transfers between devices, on_device(): lax.all_to_all(cotangent_grid, 'cz', split_axis=3, concat_axis=0, tiled=T...  14 us
    dot_general x1, matrix products, on_device(): jnp.einsum('xm,yfmz->fyzx', hartley, piece[:, :field_count], preferred_el...  12.7 us
  transfers between devices with their start and end apart: 2, of which 2 were waited for; matrix products, arithmetic and copies ran while one was open for 2% of the time, Pallas kernels for 0%

commit v1 on v0

--- a/solution.py
+++ b/solution.py
@@ -8,6 +8,22 @@
 MZ = 768
 NX = 768
 Y = 16
+
+
+def pack_series_all(x0, dim_at, target):
+    now = x0.shape
+    b_next = x0.reshape(*now[:dim_at], target, now[dim_at] // target, *now[dim_at + 1 :])
+    z2 = jnp.moveaxis(b_next, dim_at, 0)
+    return z2
+
+
+def post_the_column(block_here, array_axis):
+    block_here = jnp.moveaxis(block_here, 0, array_axis)
+    newest = block_here.shape
+    new = block_here.reshape(
+        *newest[:array_axis], newest[array_axis] * newest[array_axis + 1], *newest[array_axis + 2 :]
+    )
+    return new
 
 
 def cosine_table():
@@ -81,7 +97,20 @@
     spectral = jnp.einsum(
         "zk,yfxz->kfxy", synthesis, returned, preferred_element_type=jnp.float32
     ).astype(jnp.bfloat16)
-    result = lax.all_to_all(spectral, "cz", split_axis=0, concat_axis=3, tiled=True)
+    back = jax.lax.axis_index("cz")
+    outer = jax.lax.axis_size("cz")
+    latest, u_next = (outer, back)
+    before = pack_series_all(spectral, 0, latest)
+    main = before
+    for no in tuple(range(1, latest)):
+        all_values, near = ((u_next + no) % latest, (u_next - no) % latest)
+        block_now = lax.dynamic_index_in_dim(before, all_values, 0)
+        tray = []
+        for dd in [*range(latest)]:
+            tray.append((dd, (dd + no) % latest))
+        a_now = jax.lax.ppermute(block_now, "cz", tray)
+        main = lax.dynamic_update_slice_in_dim(main, a_now, near, axis=0)
+    result = post_the_column(main, 3)
     return result.reshape(local_modes, field_count, local_columns * Y)
 
 

time: 444 us -> 432 us (0.973)
  the two profiles are of different devices: /device:TPU:0 before, /device:TPU:1 now
where the time goes in v1:
time: 432 us; the launch traced here: 424 us
  blocking collectives  144 us (33%)
  waiting for transfers between devices  113 us (26%)
  matrix products  76.8 us (18%)
  local copies, waits for them, and re-layouts  69.3 us (16%)
  starting transfers between devices  16.7 us (4%)
    all_to_all x1, blocking collectives, on_device(): lax.all_to_all(lifted, 'kx', split_axis=3, concat_axis=2, tiled=True)  144 us
    all_to_all x1, waiting for transfers between devices, on_device(): lax.all_to_all(turned, 'kx', split_axis=2, concat_axis=3, tiled=True)  69.2 us
    dot_general x1, matrix products, on_device(): jnp.einsum('xm,yfmz->fyzx', hartley, piece[:, :field_count], preferred_el...  25.5 us
    all_to_all x2, local copies, waits for them, and re-layouts, on_device(): lax.all_to_all(lifted, 'kx', split_axis=3, concat_axis=2, tiled=True)  17.5 us
    ppermute x3, waiting for transfers between devices, on_device(): a_now = jax.lax.ppermute(block_now, 'cz', tray)  16.3 us
    all_to_all x1, waiting for transfers between devices, on_device(): lax.all_to_all(cotangent_grid, 'cz', split_axis=3, concat_axis=0, tiled=T...  14.3 us
    all_to_all x1, waiting for transfers between devices, on_device(): lax.all_to_all(field_grid, 'cz', split_axis=3, concat_axis=0, tiled=True)  13.1 us
    dot_general x1, matrix products, on_device(): jnp.einsum('xm,yfmz->fyzx', hartley, piece[:, field_count:], preferred_el...  12.7 us
  transfers between devices with their start and end apart: 6, of which 6 were waited for; matrix products, arithmetic and copies ran while one was open for 2% of the time, Pallas kernels for 0%

profile of v1, /device:TPU:1, one launch (start us, length us, event | category | flops | bytes accessed | tf_op | source)
XLA Modules:
  0.0 423.8 jit_solution(9882286519032256627)
XLA Ops:
  0.0 3.0 copy.25
  4.5 4.3 %all-to-all-start.1 = ((bf16[128,4,96,16]{0,2,1,3:T(8,128)(2,1)}), bf16[128,4,96,16]{0,2,1,3:T(8,128)(2,1)S(1)}, u32[]{:S(2)}, u32[]{:S(2)}) async-start(bf16[128,4,96,16]{0,2,1,3:T(8,128)(2,1)} %copy.26), calls=%async_computation.1 | async-start | bytes 3145728 | tf_op jit(solution)/shard_map/all_to_all | solution.py:79
  8.8 3.0 copy.21
  11.8 1.6 copy.22
  13.3 14.3 %all-to-all-done.1 = bf16[128,4,96,16]{0,2,1,3:T(8,128)(2,1)S(1)} async-done(((bf16[128,4,96,16]{0,2,1,3:T(8,128)(2,1)}), bf16[128,4,96,16]{0,2,1,3:T(8,128)(2,1)S(1)}, u32[]{:S(2)}, u32[]{:S(2)}) %all-to-all-start.1) | async-done | bytes 1572896 | tf_op jit(solution)/shard_map/all_to_all | solution.py:79
  27.6 4.8 %all-to-all-start = ((bf16[128,4,96,16]{0,2,1,3:T(8,128)(2,1)}), bf16[128,4,96,16]{0,2,1,3:T(8,128)(2,1)S(1)}, u32[]{:S(2)}, u32[]{:S(2)}) async-start(bf16[128,4,96,16]{0,2,1,3:T(8,128)(2,1)} %copy.22), calls=%async_computation | async-start | bytes 3145728 | tf_op jit(solution)/shard_map/all_to_all | solution.py:73
  32.4 2.4 copy.28
  34.7 3.7 all_to_all.59
  38.4 13.1 %all-to-all-done = bf16[128,4,96,16]{0,2,1,3:T(8,128)(2,1)S(1)} async-done(((bf16[128,4,96,16]{0,2,1,3:T(8,128)(2,1)}), bf16[128,4,96,16]{0,2,1,3:T(8,128)(2,1)S(1)}, u32[]{:S(2)}, u32[]{:S(2)}) %all-to-all-start) | async-done | bytes 1572896 | tf_op jit(solution)/shard_map/all_to_all | solution.py:73
  52.7 2.0 all_to_all.55
  54.7 9.7 %convert_bitcast_fusion.1 = bf16[4,4,96,768]{3,2,0,1:T(8,128)(2,1)S(1)} fusion(bf16[512,4,96,4]{0,2,3,1:T(8,128)(2,1)S(1)} %copy-done.1, s32[768]{0:T(1024)S(1)} %multiply_add_fusion), kind=kOutput, calls=%fused_computation.15 | convolution fusion | flops 1213464576 | bytes 3935232 | tf_op jit(solution)/shard_map/zk,kfxy->yfxz/dot_general | solution.py:76
  64.4 9.7 %convert_bitcast_fusion.2 = bf16[4,4,96,768]{3,2,0,1:T(8,128)(2,1)S(1)} fusion(bf16[512,4,96,4]{0,2,3,1:T(8,128)(2,1)S(1)} %copy-done.2, s32[768]{0:T(1024)S(1)} %multiply_add_fusion), kind=kOutput, calls=%fused_computation.16 | convolution fusion | flops 1213464576 | bytes 3935232 | tf_op jit(solution)/shard_map/zk,kfxy->yfxz/dot_general | solution.py:70
  74.1 2.6 pad_maximum_fusion
  76.8 10.9 %copy.29 = bf16[4,8,96,768]{2,0,1,3:T(4,128)(2,1)} copy(bf16[4,8,96,768]{3,2,0,1:T(8,128)(2,1)} %pad_maximum_fusion) | data formatting | bytes 9437184 | tf_op jit(solution)/shard_map/concatenate | solution.py:68
  87.7 144.0 %all_to_all.72 = bf16[4,8,96,768]{2,0,1,3:T(4,128)(2,1)S(1)} all-to-all(bf16[4,8,96,768]{2,0,1,3:T(4,128)(2,1)} %copy.29), channel_id=1, replica_groups=mesh['kx'=8,'cz'=4] {'kx'}, dimensions={3} | all-to-all | bytes 9437184 | tf_op jit(solution)/shard_map/all_to_all | solution.py:85
  231.7 6.7 %copy.50 = bf16[4,8,96,8,96]{2,3,4,1,0:T(8,128)(2,1)} copy(bf16[4,8,96,8,96]{2,0,1,4,3:T(4,128)(2,1)S(1)} %bitcast.68) | data formatting | bytes 9437184 | tf_op jit(solution)/shard_map/all_to_all | solution.py:85
  238.4 10.8 %all_to_all.63 = bf16[4,8,768,96]{2,3,1,0:T(8,128)(2,1)} reshape(bf16[4,8,8,96,96]{3,2,4,1,0:T(8,128)(2,1)} %bitcast.69) | data formatting | bytes 9437184 | tf_op jit(solution)/shard_map/all_to_all | solution.py:85
  249.3 12.7 %convolution_bitcast_fusion.1 = f32[4,4,96,768]{3,2,0,1:T(8,128)S(1)} fusion(bf16[4,8,768,96]{2,3,1,0:T(8,128)(2,1)} %all_to_all.63), kind=kOutput, calls=%fused_computation.19 | convolution fusion | flops 1819017216 | bytes 9437184 | tf_op jit(solution)/shard_map/xm,yfmz->fyzx/dot_general | solution.py:89
  262.0 25.5 %convolution_bitcast_fusion = f32[4,4,96,768]{3,2,0,1:T(8,128)S(1)} fusion(bf16[4,8,768,96]{2,3,1,0:T(8,128)(2,1)S(1)} %copy-done), kind=kOutput, calls=%fused_computation.18 | convolution fusion | flops 1819017216 | bytes 9437184 | tf_op jit(solution)/shard_map/xm,yfmz->fyzx/dot_general | solution.py:86
  288.3 10.9 %convert_bitcast_fusion = bf16[4,4,768,96]{2,3,0,1:T(8,128)(2,1)S(1)} fusion(bf16[1,4,96,768]{3,2,0,1:T(8,128)(2,1)S(1)} %get-tuple-element.6, bf16[1,4,96,768]{3,2,0,1:T(8,128)(2,1)S(1)} %get-tuple-element.7, bf16[1,4,96,768]{3,2,0,1:T(8,128)(2,1)S(1)} %get-tuple-element.8, bf16[1,4,96,768]{3,2,0,1:T(8,128)(2,1)S(1)} %get-tuple-element.5), kind=kOutput, calls=%fused_computation.10 | convolution fusion | flops 1823735808 | bytes 4718592 | tf_op jit(solution)/shard_map/xm,fyzx->yfmz/dot_general | solution.py:93
  299.3 4.5 %copy.32 = bf16[4,4,768,96]{3,0,1,2:T(4,128)(2,1)} copy(bf16[4,4,768,96]{2,3,0,1:T(8,128)(2,1)S(1)} %convert_bitcast_fusion) | data formatting | bytes 4718592 | tf_op jit(solution)/shard_map/convert_element_type | solution.py:95
  303.8 3.8 all-to-all-start.3
  307.6 69.2 %all-to-all-done.3 = bf16[4,4,768,96]{3,0,1,2:T(4,128)(2,1)S(1)} async-done(((bf16[4,4,768,96]{3,0,1,2:T(4,128)(2,1)}), bf16[4,4,768,96]{3,0,1,2:T(4,128)(2,1)S(1)}, u32[]{:S(2)}, u32[]{:S(2)}) %all-to-all-start.3) | async-done | bytes 2359328 | tf_op jit(solution)/shard_map/all_to_all | solution.py:96
  376.9 3.7 copy.51
  380.5 5.0 %all_to_all.67 = bf16[4,4,96,768]{3,2,1,0:T(8,128)(2,1)S(1)} reshape(bf16[4,4,96,8,96]{4,3,2,1,0:T(8,128)(2,1)} %bitcast.71) | data formatting | bytes 4718592 | tf_op jit(solution)/shard_map/all_to_all | solution.py:96
  385.5 8.3 %fusion.15 = bf16[512,4,96,4]{0,2,1,3:T(8,128)(2,1)} fusion(bf16[4,4,96,768]{3,2,1,0:T(8,128)(2,1)S(1)} %all_to_all.67, s32[768]{0:T(1024)S(1)} %multiply_add_fusion), kind=kOutput, calls=%fused_computation.30 | convolution fusion | flops 1213071360 | bytes 3935232 | tf_op jit(solution)/shard_map/zk,yfxz->kfxy/dot_general | solution.py:97
  393.8 2.6 reshape.18
  396.4 2.0 copy.35
  399.0 2.9 collective-permute-start
  402.8 7.3 %collective-permute-done = bf16[1,128,4,96,4]{1,4,0,3,2:T(4,128)(2,1)} collective-permute-done((bf16[1,128,4,96,4]{1,4,0,3,2:T(4,128)(2,1)S(1)}, bf16[1,128,4,96,4]{1,4,0,3,2:T(4,128)(2,1)}, u32[]{:S(2)}, u32[]{:S(2)}) %collective-permute-start) | collective-permute-done | bytes 393248 | tf_op jit(solution)/shard_map/ppermute | solution.py:111
  411.4 8.5 %collective-permute-done.1 = bf16[1,128,4,96,4]{1,4,0,3,2:T(4,128)(2,1)S(1)} collective-permute-done((bf16[1,128,4,96,4]{1,4,0,3,2:T(4,128)(2,1)S(1)}, bf16[1,128,4,96,4]{1,4,0,3,2:T(4,128)(2,1)S(1)}, u32[]{:S(2)}, u32[]{:S(2)}) %collective-permute-start.1) | collective-permute-done | bytes 393248 | tf_op jit(solution)/shard_map/ppermute | solution.py:111
  420.9 2.5 copy.38
  (17 shorter events, 7.3 us)
Async XLA Ops:
  4.5 23.1 %all-to-all-start.1 = ((bf16[128,4,96,16]{0,2,1,3:T(8,128)(2,1)}), bf16[128,4,96,16]{0,2,1,3:T(8,128)(2,1)S(1)}, u32[]{:S(2)}, u32[]{:S(2)}) async-start(bf16[128,4,96,16]{0,2,1,3:T(8,128)(2,1)} %copy.26), calls=%async_computation.1 | async-start | bytes 3145728 | tf_op jit(solution)/shard_map/all_to_all | solution.py:79
  27.6 23.8 %all-to-all-start = ((bf16[128,4,96,16]{0,2,1,3:T(8,128)(2,1)}), bf16[128,4,96,16]{0,2,1,3:T(8,128)(2,1)S(1)}, u32[]{:S(2)}, u32[]{:S(2)}) async-start(bf16[128,4,96,16]{0,2,1,3:T(8,128)(2,1)} %copy.22), calls=%async_computation | async-start | bytes 3145728 | tf_op jit(solution)/shard_map/all_to_all | solution.py:73
  52.7 2.0 copy-start.1
  54.7 9.7 %copy-start.2 = (bf16[512,4,96,4]{0,2,3,1:T(8,128)(2,1)S(1)}, bf16[512,4,96,4]{0,2,3,1:T(8,128)(2,1)}, u32[]{:S(2)}) copy-start(bf16[512,4,96,4]{0,2,3,1:T(8,128)(2,1)} %all_to_all.55) | copy-start | bytes 4718596
  249.3 12.7 %copy-start = (bf16[4,8,768,96]{2,3,1,0:T(8,128)(2,1)S(1)}, bf16[4,8,768,96]{2,3,1,0:T(8,128)(2,1)}, u32[]{:S(2)}) copy-start(bf16[4,8,768,96]{2,3,1,0:T(8,128)(2,1)} %all_to_all.63) | copy-start | bytes 14155780
  303.8 73.1 %all-to-all-start.3 = ((bf16[4,4,768,96]{3,0,1,2:T(4,128)(2,1)}), bf16[4,4,768,96]{3,0,1,2:T(4,128)(2,1)S(1)}, u32[]{:S(2)}, u32[]{:S(2)}) async-start(bf16[4,4,768,96]{3,0,1,2:T(4,128)(2,1)} %copy.32), calls=%async_computation.3 | async-start | bytes 6291456 | tf_op jit(solution)/shard_map/all_to_all | solution.py:96
  399.0 11.2 %collective-permute-start = (bf16[1,128,4,96,4]{1,4,0,3,2:T(4,128)(2,1)S(1)}, bf16[1,128,4,96,4]{1,4,0,3,2:T(4,128)(2,1)}, u32[]{:S(2)}, u32[]{:S(2)}) collective-permute-start(bf16[1,128,4,96,4]{1,4,0,3,2:T(4,128)(2,1)S(1)} %get-tuple-element.11), channel_id=1, source_target_pairs={{0,1},{1,2},{2,3},{3,0},{4,5},{5,6},{6,7},{7,4},{8,9},{9,10},{10,1... | collective-permute-start | bytes 1179656 | tf_op jit(solution)/shard_map/ppermute | solution.py:111
  401.8 18.1 %collective-permute-start.1 = (bf16[1,128,4,96,4]{1,4,0,3,2:T(4,128)(2,1)S(1)}, bf16[1,128,4,96,4]{1,4,0,3,2:T(4,128)(2,1)S(1)}, u32[]{:S(2)}, u32[]{:S(2)}) collective-permute-start(bf16[1,128,4,96,4]{1,4,0,3,2:T(4,128)(2,1)S(1)} %get-tuple-element.10), channel_id=1, source_target_pairs={{0,2},{1,3},{2,0},{3,1},{4,6},{5,7},{6,4},{7,5},{8,10},{9,11},{10,... | collective-permute-start | bytes 1179656 | tf_op jit(solution)/shard_map/ppermute | solution.py:111
  402.8 17.8 %collective-permute-start.2 = (bf16[1,128,4,96,4]{1,4,0,3,2:T(4,128)(2,1)S(1)}, bf16[1,128,4,96,4]{1,4,0,3,2:T(4,128)(2,1)S(1)}, u32[]{:S(2)}, u32[]{:S(2)}) collective-permute-start(bf16[1,128,4,96,4]{1,4,0,3,2:T(4,128)(2,1)S(1)} %get-tuple-element.9), channel_id=1, source_target_pairs={{0,3},{1,0},{2,1},{3,2},{4,7},{5,4},{6,5},{7,6},{8,11},{9,8},{10,9... | collective-permute-start | bytes 1179656 | tf_op jit(solution)/shard_map/ppermute | solution.py:111
